TPU v7x, 32 devices: a whole 2x2x4 slice. The times are simulated.
32 devices in a mesh: lat: 4 (over x, core), lon: 8 (over z, y).
Axes of the slice: x: 2, y: 2, z: 4, core: 2. Of those that a mesh axis runs over, the one named last changes fastest.
Arguments:
- node_latent: bfloat16 [64, 256, 512], P('lat', 'lon'), may hold values from -6 to 6
- edge_latent: bfloat16 [65536, 512], P(('lat', 'lon')), may hold values from -6 to 6
- sender: int32 [65536], P(('lat', 'lon')), may hold values from -1 to 16383, as said below
- receiver: int32 [65536], P(('lat', 'lon')), may hold values from -1 to 127, as said below
- block_tile: int32 [512], P(('lat', 'lon')), may hold values from 0 to 3, as said below
- w_first: bfloat16 [1536, 512], replicated, may hold values from -0.15625 to 0.15625
- w_second: bfloat16 [512, 512], replicated, may hold values from -0.25 to 0.25
- edge_gain: float32 [512], replicated, may hold values from 0.5 to 1.5
- w_node_first: bfloat16 [1024, 512], replicated, may hold values from -0.1875 to 0.1875
- w_node_second: bfloat16 [512, 512], replicated, may hold values from -0.25 to 0.25
- node_gain: float32 [512], replicated, may hold values from 0.5 to 1.5
Outputs:
- node_out: bfloat16 [64, 256, 512], P('lat', 'lon')
- edge_out: bfloat16 [65536, 512], P(('lat', 'lon'))
Inputs may be any that keep to these rules, and one draw needn't show every extreme that they name: `sender`: -1 on padded slots; otherwise the id of one of the eight grid neighbours of the edge's receiver node (columns wrap around, rows do not), or of a node whose row and column are both multiples of 4, anywhere on the grid. `receiver`: padded slots (-1) stand at the end of each block, at least 32 slots of a block are live, and live values never fall within a block. `block_tile`: never falls from one block of a device to the next, over the device's 16 blocks.
All inputs are finite; a program needn't handle non-finite values.
Results may differ from a plain program's by a relative error of at most 0.008.
Values may be sent and summed in bfloat16 or wider, within the bound.
A program may use at most 128 MiB of HBM per device.

v0:
```python
import functools

import jax
import jax.numpy as jnp
from jax import lax
from jax.experimental import pallas as pl
from jax.experimental.pallas import tpu as pltpu
from jax.sharding import PartitionSpec as P

F32 = jnp.float32
BF16 = jnp.bfloat16
LANES = 128


def dot(a, b):
    return jnp.dot(a, b, preferred_element_type=F32)


def silu(value):
    half = 0.5 * value
    return half * (1.0 + jnp.tanh(half))


def layer_norm(values, gain_vec):
    average = jnp.mean(values, -1, keepdims=True)
    centred = values - average
    spread = jnp.mean(centred * centred, -1, keepdims=True)
    return centred * lax.rsqrt(spread + 1e-05) * gain_vec


def compute_kernel(
    group,
    block_len,
    tile_nodes,
    tile_ref,
    edge_ref,
    send_ref,
    recv_ref,
    table_ref,
    own_ref,
    w_first_ref,
    w_second_ref,
    edge_gain_ref,
    w_node_first_ref,
    w_node_second_ref,
    node_gain_ref,
    node_out_ref,
    edge_out_ref,
    total_ref,
):
    step = pl.program_id(0)
    features = edge_ref.shape[1]
    node_count = own_ref.shape[0]
    table_len = node_count + table_ref.shape[0]

    @pl.when(step == 0)
    def _():
        total_ref[...] = jnp.zeros_like(total_ref)

    def columns_of(row, width):
        spread = jnp.broadcast_to(row, (LANES, block_len)).T
        lane = lax.broadcasted_iota(jnp.int32, (block_len, LANES), 1)
        parts = [
            jnp.where(spread == lane + j * LANES, 1.0, 0.0).astype(BF16)
            for j in range(width // LANES)
        ]
        return spread, jnp.concatenate(parts, axis=1)

    sent, received, live = [], [], []
    for i in range(group):
        _, hot = columns_of(send_ref[i], table_len)
        sent.append(hot)
        tile = tile_ref[step * group + i]
        start = pl.multiple_of(tile * tile_nodes, tile_nodes)
        spread, hot_recv = columns_of(recv_ref[i], tile_nodes)
        live.append(jnp.concatenate([spread] * (features // LANES), axis=1))
        received.append(dot(hot_recv, own_ref[pl.ds(start, tile_nodes), :]).astype(BF16))
    edges = edge_ref[...]
    sent = jnp.concatenate(sent, axis=0)
    send_rows = (
        dot(sent[:, :node_count], own_ref[...]) + dot(sent[:, node_count:], table_ref[...])
    ).astype(BF16)
    recv_rows = jnp.concatenate(received, axis=0)
    first = (
        dot(edges, w_first_ref[:features, :])
        + dot(recv_rows, w_first_ref[2 * features :, :])
        + dot(send_rows, w_first_ref[features : 2 * features, :])
    )
    hidden = silu(first).astype(BF16)
    message = layer_norm(dot(hidden, w_second_ref[...]), edge_gain_ref[...]).astype(BF16)
    updated = edges.astype(F32) + message.astype(F32)
    edge_out_ref[...] = jnp.where(jnp.concatenate(live, axis=0) >= 0, updated, 0.0).astype(BF16)
    for i in range(group):
        tile = tile_ref[step * group + i]
        start = pl.multiple_of(tile * tile_nodes, tile_nodes)
        node = lax.broadcasted_iota(jnp.int32, (tile_nodes, block_len), 0)
        hot = jnp.where(node == recv_ref[i], 1.0, 0.0).astype(BF16)
        total_ref[pl.ds(start, tile_nodes), :] += dot(
            hot, message[i * block_len : (i + 1) * block_len, :]
        )

    @pl.when(step == pl.num_programs(0) - 1)
    def _():
        own = own_ref[...]
        node_first = dot(own, w_node_first_ref[:features, :]) + dot(
            total_ref[...].astype(BF16), w_node_first_ref[features:, :]
        )
        node_hidden = silu(node_first).astype(BF16)
        node_second = dot(node_hidden, w_node_second_ref[...])
        node_out_ref[...] = (
            own.astype(F32) + layer_norm(node_second, node_gain_ref[...])
        ).astype(BF16)


def compute(
    block_tile, edges, senders, receivers, table, own, weights, tile_nodes
):
    blocks = block_tile.shape[0]
    edge_count, features = edges.shape
    block_len = edge_count // blocks
    node_count = own.shape[0]
    group = 4 if blocks % 4 == 0 else 1
    whole = pl.BlockSpec(memory_space=pltpu.VMEM)
    index = pl.BlockSpec((group, 1, block_len), lambda i, tiles: (i, 0, 0))
    rows = pl.BlockSpec((group * block_len, features), lambda i, tiles: (i, 0))
    return pl.pallas_call(
        functools.partial(compute_kernel, group, block_len, tile_nodes),
        grid_spec=pltpu.PrefetchScalarGridSpec(
            num_scalar_prefetch=1,
            grid=(blocks // group,),
            in_specs=[rows, index, index] + [whole] * 8,
            out_specs=[pl.BlockSpec((node_count, features), lambda i, tiles: (0, 0)), rows],
            scratch_shapes=[pltpu.VMEM((node_count, features), F32)],
        ),
        out_shape=[
            jax.ShapeDtypeStruct((node_count, features), BF16),
            jax.ShapeDtypeStruct((edge_count, features), BF16),
        ],
        compiler_params=pltpu.CompilerParams(
            dimension_semantics=("arbitrary",), vmem_limit_bytes=50 * 1024 * 1024
        ),
    )(
        block_tile,
        edges,
        senders.reshape(blocks, 1, block_len),
        receivers.reshape(blocks, 1, block_len),
        table,
        own,
        *weights,
    )


def border_rows(own, patch_rows, patch_cols):
    count = patch_rows * patch_cols
    coarse_rows, coarse_cols = patch_rows // 4, patch_cols // 4
    coarse = coarse_rows * coarse_cols
    pick = lax.broadcasted_iota(jnp.int32, (coarse + 2 * patch_rows, count), 0)
    node = lax.broadcasted_iota(jnp.int32, (coarse + 2 * patch_rows, count), 1)
    from_coarse = pick // coarse_cols * 4 * patch_cols + pick % coarse_cols * 4
    side = pick - coarse
    from_side = jnp.where(
        side < patch_rows, side * patch_cols, (side - patch_rows) * patch_cols + patch_cols - 1
    )
    hot = (node == jnp.where(pick < coarse, from_coarse, from_side)).astype(BF16)
    return dot(hot, own).astype(BF16)


def per_device(
    node_latent,
    edge_latent,
    sender,
    receiver,
    block_tile,
    w_first,
    w_second,
    edge_gain,
    w_node_first,
    w_node_second,
    node_gain,
):
    patch_rows, patch_cols, features = node_latent.shape
    lat_count, lon_count = lax.axis_size("lat"), lax.axis_size("lon")
    lat_index, lon_index = lax.axis_index("lat"), lax.axis_index("lon")
    grid_cols = patch_cols * lon_count
    node_count = patch_rows * patch_cols
    coarse_per = patch_rows // 4 * (patch_cols // 4)
    own = node_latent.reshape(node_count, features)
    picked = border_rows(own, patch_rows, patch_cols)
    near, table_len = table_layout(patch_rows, patch_cols, coarse_per * lat_count * lon_count)
    table = build_table(own, picked, patch_rows, patch_cols, near, table_len)

    send_row, send_col = sender // grid_cols, sender % grid_cols
    row = send_row - lat_index * patch_rows
    col = (send_col - lon_index * patch_cols + 1) % grid_cols - 1
    is_near = (row >= -1) & (row <= patch_rows) & (col <= patch_cols)
    inside = (col >= 0) & (col < patch_cols)
    left, right, top, bottom, corners, coarse_at = near
    side = jnp.where(col < 0, left, right)
    corner_side = jnp.where(col < 0, 0, 16)
    top_index = jnp.where(inside, top + col, corners + corner_side + 7)
    bottom_index = jnp.where(inside, bottom + col, corners + corner_side + 8)
    middle = jnp.where(inside, row * patch_cols + col, side + row)
    near_index = jnp.where(row < 0, top_index, jnp.where(row >= patch_rows, bottom_index, middle))
    far_index = (
        coarse_at
        + (send_row // patch_rows * lon_count + send_col // patch_cols) * coarse_per
        + send_row % patch_rows // 4 * (patch_cols // 4)
        + send_col % patch_cols // 4
    )
    senders = jnp.where(sender < 0, -1, jnp.where(is_near, near_index, far_index))
    weights = (
        w_first,
        w_second,
        edge_gain.reshape(1, -1),
        w_node_first,
        w_node_second,
        node_gain.reshape(1, -1),
    )
    node_out, edge_out = compute(
        block_tile, edge_latent, senders, receiver, table, own, weights, 4 * patch_cols
    )
    return node_out.reshape(patch_rows, patch_cols, features), edge_out


def table_layout(patch_rows, patch_cols, coarse_count):
    left = patch_rows * patch_cols
    right = left + patch_rows
    top = right + patch_rows
    bottom = top + patch_cols
    corners = bottom + patch_cols
    coarse_at = corners + 32
    table_len = -(-(coarse_at + coarse_count) // LANES) * LANES
    return (left, right, top, bottom, corners, coarse_at), table_len


def exchange_kernel(patch_rows, patch_cols, near, own_ref, picked_ref, table_ref, *sems):
    halo_send, halo_recv, far_send, far_recv, pair_send, pair_recv, ready = sems
    lat_count, lon_count = lax.axis_size("lat"), lax.axis_size("lon")
    lat, lon = lax.axis_index("lat"), lax.axis_index("lon")
    node_count = own_ref.shape[0]
    left, right, top, bottom, corners, coarse_at = near
    per = picked_ref.shape[0] - 2 * patch_rows
    cores = 2 if lat_count % 2 == 0 else 1
    chips = lat_count * lon_count // cores
    core = lax.rem(lat, cores)
    chip = lax.div(lat, cores) * lon_count + lon

    def place(which, on_core):
        return lax.div(which, lon_count) * cores + on_core, lax.rem(which, lon_count)

    def slot(which, on_core):
        at_lat, at_lon = place(which, on_core)
        start = coarse_at + (at_lat * lon_count + at_lon) * per
        return table_ref.at[pl.ds(pl.multiple_of(start, 8), per), :]

    def copy(source, target, send_sem, recv_sem, at_lat, at_lon):
        return pltpu.make_async_remote_copy(
            src_ref=source,
            dst_ref=target,
            send_sem=send_sem,
            recv_sem=recv_sem,
            device_id={"lat": at_lat, "lon": at_lon},
            device_id_type=pl.DeviceIdType.MESH,
        )

    coarse_own = picked_ref.at[pl.ds(0, per), :]

    def far_out(k):
        at_lat, at_lon = place(lax.rem(chip + k, chips), core)
        return copy(coarse_own, slot(chip, core), far_send.at[k], far_recv.at[k], at_lat, at_lon)

    def far_in(k):
        origin = lax.rem(chip + chips - k, chips)
        at_lat, at_lon = place(origin, core)
        return copy(coarse_own, slot(origin, core), far_send.at[k], far_recv.at[k], at_lat, at_lon)

    def pair(k, source_core):
        origin = lax.rem(chip + chips - k, chips)
        block = slot(origin, source_core)
        return copy(block, block, pair_send.at[k], pair_recv.at[k], lat + 1 - 2 * core, lon)

    first, last = per, per + patch_rows
    halos = (
        (picked_ref, last, patch_rows, left, 0, 1),
        (picked_ref, first, patch_rows, right, 0, -1),
        (own_ref, node_count - patch_cols, patch_cols, top, 1, 0),
        (own_ref, 0, patch_cols, bottom, -1, 0),
        (picked_ref, last + patch_rows - 8, 8, corners, 1, 1),
        (picked_ref, last, 8, corners + 8, -1, 1),
        (picked_ref, first + patch_rows - 8, 8, corners + 16, 1, -1),
        (picked_ref, first, 8, corners + 24, -1, -1),
    )

    def halo(i):
        ref, start, size, target, step_lat, step_lon = halos[i]
        at_lat = lax.rem(lat + step_lat + lat_count, lat_count)
        at_lon = lax.rem(lon + step_lon + lon_count, lon_count)
        return copy(
            ref.at[start : start + size, :],
            table_ref.at[target : target + size, :],
            halo_send.at[i],
            halo_recv.at[i],
            at_lat,
            at_lon,
        )

    def sends(i):
        there = lat + halos[i][4]
        return (there >= 0) & (there < lat_count)

    def receives(i):
        origin = lat - halos[i][4]
        return (origin >= 0) & (origin < lat_count)

    lax.fori_loop(1, chips, lambda k, c: (far_out(k).start(), c)[1], 0)
    if cores == 2:
        own_pair = copy(
            coarse_own, slot(chip, core), pair_send.at[0], pair_recv.at[0], lat + 1 - 2 * core, lon
        )
        own_pair.start()
    for i in range(len(halos)):
        pl.when(sends(i))(lambda i=i: halo(i).start())

    local = pltpu.make_async_copy(coarse_own, slot(chip, core), ready)
    local.start()
    for i, (_, _, size, target, _, _) in enumerate(halos):

        @pl.when(jnp.logical_not(receives(i)))
        def _():
            table_ref[target : target + size, :] = jnp.zeros((size, table_ref.shape[1]), BF16)

    used = coarse_at + lat_count * lon_count * per
    if used < table_ref.shape[0]:
        table_ref[used:, :] = jnp.zeros((table_ref.shape[0] - used, table_ref.shape[1]), BF16)

    def relay(k, c):
        far_in(k).wait_recv()
        if cores == 2:
            pair(k, core).start()
        return c

    lax.fori_loop(1, chips, relay, 0)
    local.wait()
    for i in range(len(halos)):
        pl.when(receives(i))(lambda i=i: halo(i).wait_recv())
        pl.when(sends(i))(lambda i=i: halo(i).wait_send())

    def finish(k, c):
        far_out(k).wait_send()
        if cores == 2:
            pair(k, core).wait_send()
            pair(k, 1 - core).wait_recv()
        return c

    lax.fori_loop(1, chips, finish, 0)
    if cores == 2:
        own_pair.wait_send()
        pair(0, 1 - core).wait_recv()


def build_table(own, picked, patch_rows, patch_cols, near, table_len):
    offset = own.shape[0]
    near = tuple(at - offset for at in near)
    chips = lax.axis_size("lat") * lax.axis_size("lon")
    sems = [pltpu.SemaphoreType.DMA((8,))] * 2 + [pltpu.SemaphoreType.DMA((chips,))] * 4
    return pl.pallas_call(
        functools.partial(exchange_kernel, patch_rows, patch_cols, near),
        in_specs=[pl.BlockSpec(memory_space=pltpu.VMEM)] * 2,
        out_specs=pl.BlockSpec(memory_space=pltpu.VMEM),
        out_shape=jax.ShapeDtypeStruct((table_len - offset, own.shape[1]), BF16),
        scratch_shapes=sems + [pltpu.SemaphoreType.DMA],
        compiler_params=pltpu.CompilerParams(
            has_side_effects=True, vmem_limit_bytes=16 * 1024 * 1024
        ),
        cost_estimate=pl.CostEstimate(
            flops=0, bytes_accessed=40 * chips * own.size // 16, transcendentals=0
        ),
    )(own, picked)


def solution(mesh):
    return jax.shard_map(
        per_device,
        mesh=mesh,
        in_specs=(
            P("lat", "lon", None),
            P(("lat", "lon"), None),
            P(("lat", "lon")),
            P(("lat", "lon")),
            P(("lat", "lon")),
            P(),
            P(),
            P(),
            P(),
            P(),
            P(),
        ),
        out_specs=(P("lat", "lon", None), P(("lat", "lon"), None)),
        check_vma=False,
    )
```

profile of v0, /device:TPU:1, one launch (start us, length us, event | category | flops | bytes accessed | tf_op | source)
XLA Modules:
  0.0 45.9 jit_solution(3187665518667449898)
XLA Ops:
  0.6 0.0 copy-start.7
  0.6 0.0 copy-start.6
  0.7 0.0 copy-start.8
  0.7 0.0 copy-start.5
  0.7 0.0 copy-start.1
  0.7 0.8 %fusion.15 = s32[2048]{0:T(1024)S(1)} fusion(s32[2048]{0:T(1024)} %param.13, s32[]{:T(128)S(6)} %mul.36, s32[]{:T(128)S(6)} %mul.35), kind=kLoop, calls=%fused_computation.45 | loop fusion | flops 278528 | bytes 16392 | tf_op jit(solution)/shard_map/jit(_where)/select_n | solution.py:210
  1.6 1.3 %convolution_convert_fusion.picked_ref = bf16[64,512]{1,0:T(8,128)(2,1)S(1)} fusion(bf16[512,512]{1,0:T(8,128)(2,1)} %bitcast.7, s32[64]{0:T(128)S(1)} %get-tuple-element.13, s32[64]{0:T(128)S(1)} %get-tuple-element.12, s32[64]{0:T(128)S(1)} %get-tuple-element.9, s32[64]{0:T(128)S(1)} %get-tuple-element.14, s32[64]{0:T(128)S(1)} %get-tuple-element.8, ...), kind=kOutput, calls=%fused_computation | convolution fusion | flops 33849344 | bytes 591616 | tf_op jit(solution)/shard_map/dot_general | solution.py:16
  2.9 0.0 copy-start
  2.9 1.0 %copy-done = bf16[16,32,512]{2,1,0:T(8,128)(2,1)S(1)} copy-done((bf16[16,32,512]{2,1,0:T(8,128)(2,1)S(1)}, bf16[16,32,512]{2,1,0:T(8,128)(2,1)}, u32[]{:S(2)}) %copy-start) | copy-done | bytes 524312
  4.0 0.0 copy-start.2
  4.0 0.0 copy-start.3
  4.0 24.3 %shard_map.122.table_ref = bf16[1152,512]{1,0:T(8,128)(2,1)S(1)} custom-call(bf16[512,512]{1,0:T(8,128)(2,1)S(1)} %bitcast.8, bf16[64,512]{1,0:T(8,128)(2,1)S(1)} %convolution_convert_fusion.picked_ref), custom_call_target="tpu_custom_call" | custom-call | bytes 20971520 | tf_op jit(solution)/shard_map/pallas_call | solution.py:366
  28.2 0.0 copy-done.7
  28.3 0.0 copy-done.6
  28.3 0.0 copy-done.8
  28.3 0.0 copy-done.5
  28.3 0.0 copy-done.1
  28.3 0.0 copy-done.2
  28.3 0.0 copy-done.3
  28.3 0.0 copy-start.4
  28.3 1.0 %copy-done.4 = bf16[512,512]{1,0:T(8,128)(2,1)S(1)} copy-done((bf16[512,512]{1,0:T(8,128)(2,1)S(1)}, bf16[512,512]{1,0:T(8,128)(2,1)}, u32[]{:S(2)}) %copy-start.4) | copy-done | bytes 524312
  29.4 16.5 %shard_map.123 = (bf16[512,512]{1,0:T(8,128)(2,1)}, bf16[2048,512]{1,0:T(8,128)(2,1)}) custom-call(s32[16]{0:T(128)S(1)} %copy-done.8, bf16[2048,512]{1,0:T(8,128)(2,1)} %edge_ref.1, s32[16,1,128]{2,1,0:T(1,128)S(1)} %bitcast.10, s32[16,1,128]{2,1,0:T(1,128)S(1)} %bitcast.11, bf16[1152,512]{1,0:T(8,128)(2,1)S(1)} %shard_map.122.table_ref, ...), custom_call_target="tpu_custom_call" | custom-call | tf_op jit(solution)/shard_map/pallas_call | solution.py:126
  (5 shorter events, 0.0 us)
Async XLA Ops:
  0.6 27.6 %copy-start.7 = (f32[512]{0:T(512)S(1)}, f32[512]{0:T(512)}, u32[]{:S(2)}) copy-start(f32[512]{0:T(512)} %param.21) | copy-start | bytes 6148
  0.6 27.6 %copy-start.6 = (f32[512]{0:T(512)S(1)}, f32[512]{0:T(512)}, u32[]{:S(2)}) copy-start(f32[512]{0:T(512)} %param.18) | copy-start | bytes 6148
  0.7 27.6 %copy-start.8 = (s32[16]{0:T(128)S(1)}, s32[16]{0:T(128)}, u32[]{:S(2)}) copy-start(s32[16]{0:T(128)} %tile_ref.1) | copy-start | bytes 196
  0.7 27.6 %copy-start.5 = (s32[2048]{0:T(1024)S(1)}, s32[2048]{0:T(1024)}, u32[]{:S(2)}) copy-start(s32[2048]{0:T(1024)} %param.14) | copy-start | bytes 24580
  0.7 27.6 %copy-start.1 = (bf16[16,32,512]{2,1,0:T(8,128)(2,1)S(1)}, bf16[16,32,512]{2,1,0:T(8,128)(2,1)}, u32[]{:S(2)}) copy-start(bf16[16,32,512]{2,1,0:T(8,128)(2,1)} %param.11) | copy-start | bytes 1572868
  2.9 1.1 %copy-start = (bf16[16,32,512]{2,1,0:T(8,128)(2,1)S(1)}, bf16[16,32,512]{2,1,0:T(8,128)(2,1)}, u32[]{:S(2)}) copy-start(bf16[16,32,512]{2,1,0:T(8,128)(2,1)} %param.11) | copy-start | bytes 1572868
  4.0 24.3 %copy-start.2 = (bf16[1024,512]{1,0:T(8,128)(2,1)S(1)}, bf16[1024,512]{1,0:T(8,128)(2,1)}, u32[]{:S(2)}) copy-start(bf16[1024,512]{1,0:T(8,128)(2,1)} %w_node_first_ref.1) | copy-start | bytes 3145732
  4.0 24.4 %copy-start.3 = (bf16[512,512]{1,0:T(8,128)(2,1)S(1)}, bf16[512,512]{1,0:T(8,128)(2,1)}, u32[]{:S(2)}) copy-start(bf16[512,512]{1,0:T(8,128)(2,1)} %w_second_ref.1) | copy-start | bytes 1572868
  28.3 1.0 %copy-start.4 = (bf16[512,512]{1,0:T(8,128)(2,1)S(1)}, bf16[512,512]{1,0:T(8,128)(2,1)}, u32[]{:S(2)}) copy-start(bf16[512,512]{1,0:T(8,128)(2,1)} %w_node_second_ref.1) | copy-start | bytes 1572868
where the time goes:
time: 46.3 us; the launch traced here: 45.9 us
  Pallas kernels  40.8 us (88%)
  local copies, waits for them, and re-layouts  2.11 us (5%)
  matrix products  1.33 us (3%)
  other arithmetic  0.85 us (2%)
  between operations  0.79 us (2%)
    pallas_call x1, Pallas kernels, build_table(): pl.pallas_call(functools.partial(exchange_kernel, patch_rows, patch_cols,...  24.3 us
    pallas_call x1, Pallas kernels, compute(): pl.pallas_call(functools.partial(compute_kernel, group, block_len, tile_n...  16.5 us
    unnamed x18, local copies, waits for them, and re-layouts  2.11 us
    dot_general x1, matrix products, dot(): return jnp.dot(a, b, preferred_element_type=F32)  1.33 us

commit v1 on v0

v1 whole, which is shorter than its diff:
```python
import functools

import jax
import jax.numpy as jnp
from jax import lax
from jax.experimental import pallas as pl
from jax.experimental.pallas import tpu as pltpu
from jax.sharding import PartitionSpec as P

F32 = jnp.float32
BF16 = jnp.bfloat16
LANES = 128
CHUNK = 32
MIB = 1024 * 1024


def dot(a, b):
    return jnp.dot(a, b, preferred_element_type=F32)


def silu(value):
    half = 0.5 * value
    return half * (1.0 + jnp.tanh(half))


def layer_norm(values, gain_vec):
    average = jnp.mean(values, -1, keepdims=True)
    centred = values - average
    spread = jnp.mean(centred * centred, -1, keepdims=True)
    return centred * lax.rsqrt(spread + 1e-05) * gain_vec


def power_of_two(n):
    return n & (n - 1) == 0


def quotient(value, n):
    if power_of_two(n):
        return lax.shift_right_arithmetic(value, jnp.full_like(value, n.bit_length() - 1))
    return lax.div(value, jnp.full_like(value, n))


def remainder(value, n):
    if power_of_two(n):
        return value & (n - 1)
    return lax.rem(value, jnp.full_like(value, n))


def plan(patch_rows, patch_cols, lat_count, lon_count):
    cores = 2 if lat_count % 2 == 0 else 1
    low = 1
    while lon_count % (4 * low) == 0 and 4 * low * low <= lon_count:
        low *= 2
    left = patch_rows * patch_cols
    right = left + patch_rows
    top = right + patch_rows
    bottom = top + patch_cols
    corners = bottom + patch_cols
    coarse_at = corners + 32
    per = patch_rows // 4 * (patch_cols // 4)
    return dict(
        cores=cores,
        wide=lat_count // cores,
        high=lon_count // low,
        low=low,
        near=(left, right, top, bottom, corners, coarse_at),
        per=per,
        length=coarse_at + per * lat_count * lon_count,
    )


def sender_rows(sender, lat, lon, patch_rows, patch_cols, lon_count, shape):
    grid_cols = patch_cols * lon_count
    left, right, top, bottom, corners, coarse_at = shape["near"]
    send_row, send_col = quotient(sender, grid_cols), remainder(sender, grid_cols)
    row = send_row - lat * patch_rows
    col = remainder(send_col - lon * patch_cols + 1 + grid_cols, grid_cols) - 1
    is_near = (row >= -1) & (row <= patch_rows) & (col <= patch_cols)
    inside = (col >= 0) & (col < patch_cols)
    side = jnp.where(col < 0, left, right)
    corner = corners + jnp.where(col < 0, 0, 16)
    top_index = jnp.where(inside, top + col, corner + 7)
    bottom_index = jnp.where(inside, bottom + col, corner + 8)
    middle = jnp.where(inside, row * patch_cols + col, side + row)
    near_index = jnp.where(row < 0, top_index, jnp.where(row >= patch_rows, bottom_index, middle))
    at_lat, at_lon = quotient(send_row, patch_rows), quotient(send_col, patch_cols)
    core, across = remainder(at_lat, shape["cores"]), quotient(at_lat, shape["cores"])
    high, low = quotient(at_lon, shape["low"]), remainder(at_lon, shape["low"])
    block = ((high * shape["cores"] + core) * shape["wide"] + across) * shape["low"] + low
    far_index = (
        coarse_at
        + block * shape["per"]
        + quotient(remainder(send_row, patch_rows), 4) * (patch_cols // 4)
        + quotient(remainder(send_col, patch_cols), 4)
    )
    return jnp.where(sender < 0, 0, jnp.where(is_near, near_index, far_index))


def border_hot(patch_rows, patch_cols, first_row, rows):
    count = patch_rows * patch_cols
    coarse_cols = patch_cols // 4
    coarse = patch_rows // 4 * coarse_cols
    pick = lax.broadcasted_iota(jnp.int32, (rows, count), 0) + first_row
    node = lax.broadcasted_iota(jnp.int32, (rows, count), 1)
    from_coarse = quotient(pick, coarse_cols) * (4 * patch_cols) + remainder(pick, coarse_cols) * 4
    side = pick - coarse
    from_side = jnp.where(
        side < patch_rows, side * patch_cols, (side - patch_rows) * patch_cols + patch_cols - 1
    )
    return jnp.where(node == jnp.where(pick < coarse, from_coarse, from_side), 1.0, 0.0).astype(BF16)


def gather_kernel(
    shape,
    patch_rows,
    patch_cols,
    tile_nodes,
    node_hbm,
    edge_hbm,
    send_hbm,
    recv_hbm,
    tile_hbm,
    w_hbm,
    first_ref,
    sent_ref,
    index_ref,
    own_ref,
    edge_ref,
    send_ref,
    recv_ref,
    tile_ref,
    w_ref,
    side_ref,
    table_ref,
    received_ref,
    load_sem,
    edge_sem,
    halo_send,
    halo_recv,
    line_send,
    line_recv,
    plane_send,
    plane_recv,
    core_send,
    core_recv,
):
    lat_count, lon_count = lax.axis_size("lat"), lax.axis_size("lon")
    lat, lon = lax.axis_index("lat"), lax.axis_index("lon")
    cores, wide, high_count, low_count = (shape[k] for k in ("cores", "wide", "high", "low"))
    per = shape["per"]
    node_count, features = own_ref.shape
    left, right, top, bottom, corners, coarse_at = (at - node_count for at in shape["near"])
    core, across = lax.rem(lat, cores), lax.div(lat, cores)
    high, low = lax.div(lon, low_count), lax.rem(lon, low_count)
    tiles = features // LANES
    blocks, block_len = recv_ref.shape

    def load(source, target, i):
        return pltpu.make_async_copy(source, target, load_sem.at[i])

    loads = [
        load(node_hbm, own_ref, 0),
        load(w_hbm, w_ref, 1),
        load(send_hbm, send_ref, 2),
        load(recv_hbm, recv_ref, 3),
        load(tile_hbm, tile_ref, 4),
    ]
    edge_load = pltpu.make_async_copy(edge_hbm, edge_ref, edge_sem)
    loads[0].start()

    def device(at_across, at_core, at_high, at_low):
        return at_across * cores + at_core, at_high * low_count + at_low

    offsets = [(a, b) for a in range(wide) for b in range(low_count)][1:]

    def turn(at, step, count):
        return lax.rem(at + step, count) if step else at

    def line_to(k):
        return device(across, core, turn(high, k, high_count), low)

    def plane_to(step):
        return device(turn(across, step[0], wide), core, high, turn(low, step[1], low_count))

    partner = device(across, 1 - core, high, low)

    last = patch_rows
    halos = (
        (side_ref, last, patch_rows, left, 0, 1),
        (side_ref, 0, patch_rows, right, 0, -1),
        (own_ref, node_count - patch_cols, patch_cols, top, 1, 0),
        (own_ref, 0, patch_cols, bottom, -1, 0),
        (side_ref, last + patch_rows - 8, 8, corners, 1, 1),
        (side_ref, last, 8, corners + 8, -1, 1),
        (side_ref, patch_rows - 8, 8, corners + 16, 1, -1),
        (side_ref, 0, 8, corners + 24, -1, -1),
    )

    def halo_to(i):
        return (
            lax.rem(lat + halos[i][4] + lat_count, lat_count),
            lax.rem(lon + halos[i][5] + lon_count, lon_count),
        )

    barrier = pltpu.get_barrier_semaphore()
    greeted = [line_to(k) for k in range(1, high_count)] + [plane_to(step) for step in offsets]
    greeted += [partner] if cores == 2 else []
    greeted += [halo_to(i) for i in range(len(halos))]
    for at in greeted:
        pl.semaphore_signal(
            barrier, inc=1, device_id=at, device_id_type=pl.DeviceIdType.MESH
        )
    for each in loads[1:]:
        each.start()
    edge_load.start()

    def slots(at_high, at_core, at_across, at_low, count=1):
        block = ((at_high * cores + at_core) * wide + at_across) * low_count + at_low
        return pl.ds(pl.multiple_of(coarse_at + block * per, 8), count * per)

    def copy(source, target, send_sem, recv_sem, at):
        return pltpu.make_async_remote_copy(
            src_ref=source,
            dst_ref=target,
            send_sem=send_sem,
            recv_sem=recv_sem,
            device_id=at,
            device_id_type=pl.DeviceIdType.MESH,
        )

    def line(k, origin):
        block = table_ref.at[slots(origin, core, across, low), :]
        return copy(block, block, line_send.at[k], line_recv.at[k], line_to(k))

    def line_out(k):
        return line(k, high)

    def line_in(k):
        return line(k, turn(high, high_count - k, high_count))

    def from_high(j):
        return turn(high, (high_count - j) % high_count, high_count)

    def plane(j, i, at_across, at_low):
        block = table_ref.at[slots(from_high(j), core, at_across, at_low), :]
        return copy(block, block, plane_send.at[j, i], plane_recv.at[j, i], plane_to(offsets[i]))

    def plane_out(j, i):
        return plane(j, i, across, low)

    def plane_in(j, i):
        a, b = offsets[i]
        return plane(
            j,
            i,
            turn(across, (wide - a) % wide, wide),
            turn(low, (low_count - b) % low_count, low_count),
        )

    def pair(j, at_core):
        block = table_ref.at[slots(from_high(j), at_core, 0, 0, wide * low_count), :]
        return copy(block, block, core_send.at[j], core_recv.at[j], partner)

    def halo(i):
        ref, start, size, target, _, _ = halos[i]
        return copy(
            ref.at[start : start + size, :],
            table_ref.at[target : target + size, :],
            halo_send.at[i],
            halo_recv.at[i],
            halo_to(i),
        )

    def sends(i):
        there = lat + halos[i][4]
        return (there >= 0) & (there < lat_count)

    def receives(i):
        origin = lat - halos[i][4]
        return (origin >= 0) & (origin < lat_count)

    coarse_hot = border_hot(patch_rows, patch_cols, 0, per)
    side_hot = border_hot(patch_rows, patch_cols, per, 2 * patch_rows)
    loads[0].wait()
    own = own_ref[...]
    table_ref[slots(high, core, across, low), :] = dot(coarse_hot, own).astype(BF16)
    side_ref[...] = dot(side_hot, own).astype(BF16)
    for i, (_, _, size, target, _, _) in enumerate(halos):

        @pl.when(jnp.logical_not(receives(i)))
        def _():
            table_ref[target : target + size, :] = jnp.zeros((size, features), BF16)

    pl.semaphore_wait(barrier, len(greeted))
    for k in range(1, high_count):
        line_out(k).start()
    for i in range(len(offsets)):
        plane_out(0, i).start()
    for i in range(len(halos)):
        pl.when(sends(i))(lambda i=i: halo(i).start())

    def relay_line(k):
        line_in(k).wait_recv()
        for i in range(len(offsets)):
            plane_out(k, i).start()

    def relay_plane(j):
        for i in range(len(offsets)):
            plane_in(j, i).wait_recv()
        if cores == 2:
            pair(j, core).start()

    def project(rows, start):
        result = dot(rows, w_ref[features : 2 * features, :])
        for t in range(tiles):
            sent_ref[pl.ds(start * tiles + t, rows.shape[0], stride=tiles), :] = result[
                :, t * LANES : (t + 1) * LANES
            ]

    def project_coarse(j):
        if cores == 2:
            pair(j, 1 - core).wait_recv()
        count = cores * wide * low_count * per
        rows = slots(from_high(j), 0, 0, 0, cores * wide * low_count)
        start = pl.multiple_of(node_count + coarse_at + from_high(j) * count, 8)
        project(table_ref[rows, :], start)

    def first_layer(g, size):
        rows = slice(g * size, (g + 1) * size)
        received = []
        for i in range(g * size // block_len, (g + 1) * size // block_len):
            local = recv_ref[i : i + 1, :] + tile_ref[i] * tile_nodes
            spread = jnp.broadcast_to(local, (LANES, block_len)).T
            lane = lax.broadcasted_iota(jnp.int32, (block_len, LANES), 1)
            parts = [
                jnp.where(spread == lane + at, 1.0, 0.0).astype(BF16)
                for at in range(0, node_count, LANES)
            ]
            received.append(jnp.concatenate(parts, axis=1))
        first_ref[rows, :] = dot(edge_ref[rows, :], w_ref[:features, :]) + dot(
            jnp.concatenate(received, axis=0), received_ref[...]
        )

    loads[2].wait()
    index_ref[...] = tiles * sender_rows(
        send_ref[...], lat, lon, patch_rows, patch_cols, lon_count, shape
    )
    loads[1].wait()
    received_ref[...] = dot(own, w_ref[2 * features :, :]).astype(BF16)
    project(own, 0)
    loads[3].wait()
    loads[4].wait()
    edge_load.wait()

    groups = 8 if blocks % 8 == 0 else 1
    size = blocks * block_len // groups
    work = [functools.partial(first_layer, g, size) for g in range(groups)]

    def do(count):
        for _ in range(min(count, len(work))):
            work.pop(0)()

    for k in range(1, high_count):
        relay_line(k)
        do(1)
    relay_plane(0)
    do(2)
    for j in range(1, high_count):
        relay_plane(j)
        do(1)
        if j == 1:
            do(len(work))
            for i in range(len(halos)):
                pl.when(receives(i))(lambda i=i: halo(i).wait_recv())
            project(table_ref[:coarse_at, :], node_count)
        project_coarse(j - 1)
    do(len(work))
    project_coarse(high_count - 1)

    for k in range(1, high_count):
        line_out(k).wait_send()
    for j in range(high_count):
        for i in range(len(offsets)):
            plane_out(j, i).wait_send()
        if cores == 2:
            pair(j, core).wait_send()
    for i in range(len(halos)):
        pl.when(sends(i))(lambda i=i: halo(i).wait_send())


def in_hbm(*arrays):
    return [pltpu.with_memory_space_constraint(each, pltpu.HBM) for each in arrays]


def gather(shape, node, edges, senders, receivers, block_tile, w_first, patch_rows, patch_cols):
    node_count, features = node.shape
    edge_count = edges.shape[0]
    blocks, block_len = receivers.shape
    tiles = features // LANES
    near = shape["near"][-1] - node_count
    high = shape["high"]
    others = max(shape["wide"] * shape["low"] - 1, 1)
    dma = pltpu.SemaphoreType.DMA
    hbm, vmem = pl.BlockSpec(memory_space=pltpu.HBM), pl.BlockSpec(memory_space=pltpu.VMEM)
    return pl.pallas_call(
        functools.partial(gather_kernel, shape, patch_rows, patch_cols, 4 * patch_cols),
        in_specs=[hbm] * 6,
        out_specs=[vmem] * 3,
        out_shape=[
            pltpu.VMEM((edge_count, features), F32),
            pltpu.VMEM((shape["length"] * tiles, LANES), F32),
            pltpu.VMEM((blocks, block_len), jnp.int32),
        ],
        scratch_shapes=[
            pltpu.VMEM((node_count, features), BF16),
            pltpu.VMEM((edge_count, features), BF16),
            pltpu.VMEM((blocks, block_len), jnp.int32),
            pltpu.VMEM((blocks, block_len), jnp.int32),
            pltpu.SMEM((blocks,), jnp.int32),
            pltpu.VMEM(w_first.shape, BF16),
            pltpu.VMEM((2 * patch_rows, features), BF16),
            pltpu.VMEM((shape["length"] - node_count, features), BF16),
            pltpu.VMEM((node_count, features), BF16),
            dma((5,)),
            dma,
            dma((8,)),
            dma((8,)),
            dma((high,)),
            dma((high,)),
            dma((high, others)),
            dma((high, others)),
            dma((high,)),
            dma((high,)),
        ],
        compiler_params=pltpu.CompilerParams(
            has_side_effects=True, collective_id=0, vmem_limit_bytes=20 * MIB
        ),
        cost_estimate=pl.CostEstimate(
            flops=8 * edge_count * features * features, bytes_accessed=8 * MIB, transcendentals=0
        ),
    )(*in_hbm(node, edges, senders, receivers, block_tile, w_first))


def update_kernel(
    group,
    tile_nodes,
    index_ref,
    first_ref,
    sent_ref,
    tile_hbm,
    edge_hbm,
    recv_hbm,
    node_hbm,
    w_second_hbm,
    edge_gain_hbm,
    w_node_first_hbm,
    w_node_second_hbm,
    node_gain_hbm,
    node_out_hbm,
    edge_out_hbm,
    tile_ref,
    edge_ref,
    recv_ref,
    own_ref,
    w_second_ref,
    edge_gain_ref,
    w_node_first_ref,
    w_node_second_ref,
    node_gain_ref,
    picked_ref,
    hidden_ref,
    second_ref,
    message_ref,
    edge_out_ref,
    total_ref,
    node_out_ref,
    load_sem,
    out_sem,
):
    edge_count, features = edge_ref.shape
    tiles = features // LANES
    block_len = recv_ref.shape[1]
    groups = edge_count // group
    pairs = (
        (w_second_hbm, w_second_ref),
        (edge_gain_hbm, edge_gain_ref),
        (edge_hbm, edge_ref),
        (recv_hbm, recv_ref),
        (tile_hbm, tile_ref),
        (node_hbm, own_ref),
        (w_node_first_hbm, w_node_first_ref),
        (w_node_second_hbm, w_node_second_ref),
        (node_gain_hbm, node_gain_ref),
    )
    loads = [
        pltpu.make_async_copy(source, target, load_sem.at[i])
        for i, (source, target) in enumerate(pairs)
    ]
    for each in loads:
        each.start()
    total_ref[...] = jnp.zeros_like(total_ref)

    def pick(g):
        slot = g % 2
        for e in range(group):
            at = g * group + e
            start = pl.multiple_of(index_ref[at // block_len, at % block_len], tiles)
            picked_ref[slot, e * tiles : (e + 1) * tiles, :] = sent_ref[pl.ds(start, tiles), :]

    def hide(g):
        slot = g % 2
        for r in range(0, group, CHUNK):
            at = g * group + r
            parts = []
            for t in range(tiles):
                first = (
                    first_ref[at : at + CHUNK, t * LANES : (t + 1) * LANES]
                    + picked_ref[slot, pl.ds(r * tiles + t, CHUNK, stride=tiles), :]
                )
                parts.append(silu(first).astype(BF16))
            hidden_ref[slot, r : r + CHUNK, :] = jnp.concatenate(parts, axis=1)

    def finish(g):
        slot = g % 2
        for i in range(group // block_len):
            block = g * (group // block_len) + i
            receiver = recv_ref[block : block + 1, :]
            spread = jnp.broadcast_to(receiver, (LANES, block_len)).T
            for r in range(i * block_len, (i + 1) * block_len, CHUNK):
                at = g * group + r
                second = second_ref[slot, r : r + CHUNK, :]
                message = layer_norm(second, edge_gain_ref[...]).astype(BF16)
                message_ref[slot, r : r + CHUNK, :] = message
                updated = edge_ref[at : at + CHUNK, :].astype(F32) + message.astype(F32)
                live = spread[r % block_len : r % block_len + CHUNK, :]
                live = jnp.concatenate([live] * tiles, axis=1)
                edge_out_ref[at : at + CHUNK, :] = jnp.where(live >= 0, updated, 0.0).astype(BF16)
            start = pl.multiple_of(tile_ref[block] * tile_nodes, tile_nodes)
            node = lax.broadcasted_iota(jnp.int32, (tile_nodes, block_len), 0)
            hot = jnp.where(node == receiver, 1.0, 0.0).astype(BF16)
            total_ref[pl.ds(start, tile_nodes), :] += dot(
                hot, message_ref[slot, i * block_len : (i + 1) * block_len, :]
            )

    def store(g):
        rows = pl.ds(g * group, group)
        return pltpu.make_async_copy(
            edge_out_ref.at[rows, :], edge_out_hbm.at[rows, :], out_sem.at[g]
        )

    for g in range(groups):
        pick(g)
        hide(g)
        if g == 0:
            loads[0].wait()
        second_ref[g % 2] = dot(hidden_ref[g % 2], w_second_ref[...])
        if g == 0:
            for each in loads[1:5]:
                each.wait()
        finish(g)
        store(g).start()

    for each in loads[5:]:
        each.wait()
    own = own_ref[...]
    node_first = dot(own, w_node_first_ref[:features, :]) + dot(
        total_ref[...].astype(BF16), w_node_first_ref[features:, :]
    )
    node_second = dot(silu(node_first).astype(BF16), w_node_second_ref[...])
    node_out_ref[...] = (
        own.astype(F32) + layer_norm(node_second, node_gain_ref[...])
    ).astype(BF16)
    node_store = pltpu.make_async_copy(node_out_ref, node_out_hbm, out_sem.at[groups])
    node_store.start()
    for g in range(groups):
        store(g).wait()
    node_store.wait()


def update(index, first, sent, block_tile, edges, receivers, node, weights, tile_nodes):
    edge_count, features = edges.shape
    node_count = node.shape[0]
    blocks, block_len = receivers.shape
    tiles = features // LANES
    group = 4 * block_len if blocks % 4 == 0 else block_len
    groups = edge_count // group
    hbm, vmem = pl.BlockSpec(memory_space=pltpu.HBM), pl.BlockSpec(memory_space=pltpu.VMEM)
    loaded = (edges, receivers, node, *weights)
    return pl.pallas_call(
        functools.partial(update_kernel, group, tile_nodes),
        in_specs=[pl.BlockSpec(memory_space=pltpu.SMEM), vmem, vmem] + [hbm] * 9,
        out_specs=[hbm, hbm],
        out_shape=[
            jax.ShapeDtypeStruct((node_count, features), BF16),
            jax.ShapeDtypeStruct((edge_count, features), BF16),
        ],
        scratch_shapes=[pltpu.SMEM((blocks,), jnp.int32)]
        + [pltpu.VMEM(each.shape, each.dtype) for each in loaded]
        + [
            pltpu.VMEM((2, group * tiles, LANES), F32),
            pltpu.VMEM((2, group, features), BF16),
            pltpu.VMEM((2, group, features), F32),
            pltpu.VMEM((2, group, features), BF16),
            pltpu.VMEM((edge_count, features), BF16),
            pltpu.VMEM((node_count, features), F32),
            pltpu.VMEM((node_count, features), BF16),
            pltpu.SemaphoreType.DMA((9,)),
            pltpu.SemaphoreType.DMA((groups + 1,)),
        ],
        compiler_params=pltpu.CompilerParams(vmem_limit_bytes=24 * MIB),
    )(index, first, sent, *in_hbm(block_tile, *loaded))


def per_device(
    node_latent,
    edge_latent,
    sender,
    receiver,
    block_tile,
    w_first,
    w_second,
    edge_gain,
    w_node_first,
    w_node_second,
    node_gain,
):
    patch_rows, patch_cols, features = node_latent.shape
    blocks = block_tile.shape[0]
    shape = plan(patch_rows, patch_cols, lax.axis_size("lat"), lax.axis_size("lon"))
    node = node_latent.reshape(patch_rows * patch_cols, features)
    receivers = receiver.reshape(blocks, -1)
    first, sent, index = gather(
        shape,
        node,
        edge_latent,
        sender.reshape(blocks, -1),
        receivers,
        block_tile,
        w_first,
        patch_rows,
        patch_cols,
    )
    weights = (
        w_second,
        edge_gain.reshape(1, -1),
        w_node_first,
        w_node_second,
        node_gain.reshape(1, -1),
    )
    node_out, edge_out = update(
        index, first, sent, block_tile, edge_latent, receivers, node, weights, 4 * patch_cols
    )
    return node_out.reshape(patch_rows, patch_cols, features), edge_out


def solution(mesh):
    return jax.shard_map(
        per_device,
        mesh=mesh,
        in_specs=(
            P("lat", "lon", None),
            P(("lat", "lon"), None),
            P(("lat", "lon")),
            P(("lat", "lon")),
            P(("lat", "lon")),
            P(),
            P(),
            P(),
            P(),
            P(),
            P(),
        ),
        out_specs=(P("lat", "lon", None), P(("lat", "lon"), None)),
        check_vma=False,
    )
```

time: 46.3 us -> 27.1 us (0.59)
  Pallas kernels: 40.8 us -> 26.3 us
  local copies, waits for them, and re-layouts: 2.11 us -> 0 us
  matrix products: 1.33 us -> 0 us
  other arithmetic: 0.85 us -> 0 us
    pallas_call x2, Pallas kernels: 40.8 us -> 26.3 us  [the longest x1 17.3 us: gather(): pl.pallas_call(functools.partial(gather_kernel, shape, patch_rows, patch_...]
    unnamed x18 -> x0, local copies, waits for them, and re-layouts: 2.11 us -> none
    dot_general x1 -> x0, matrix products: 1.33 us -> none  [dot(): return jnp.dot(a, b, preferred_element_type=F32)]
    select_n x1 -> x0, other arithmetic: 0.82 us -> none  [per_device(): jnp.where(sender < 0, -1, jnp.where(is_near, near_index, far_index))]
where the time goes in v1:
time: 27.1 us; the launch traced here: 26.9 us
  Pallas kernels  26.3 us (97%)
  between operations  0.64 us (2%)
    pallas_call x1, Pallas kernels, gather(): pl.pallas_call(functools.partial(gather_kernel, shape, patch_rows, patch_...  17.3 us
    pallas_call x1, Pallas kernels, update(): pl.pallas_call(functools.partial(update_kernel, group, tile_nodes), in_sp...  8.98 us

profile of v1, /device:TPU:1, one launch (start us, length us, event | category | flops | bytes accessed | tf_op | source)
XLA Modules:
  0.0 26.9 jit_solution(5421679967663810242)
XLA Ops:
  0.6 17.3 %shard_map.122 = (f32[2048,512]{1,0:T(8,128)S(1)}, f32[6656,128]{1,0:T(8,128)S(1)}, s32[16,128]{1,0:T(8,128)S(1)}) custom-call(bf16[512,512]{1,0:T(8,128)(2,1)} %bitcast.6, bf16[2048,512]{1,0:T(8,128)(2,1)} %edge_hbm.3, s32[16,128]{1,0:T(8,128)} %bitcast.13, s32[16,128]{1,0:T(8,128)} %bitcast.8, s32[16]{0:T(128)} %tile_hbm.3, bf16[1536,512]{1,0:T(8,128)(2,1)} %w_hbm.1), custom_call_target="tpu_custom_call" | custom-call | flops 4294967296 | bytes 8388608 | tf_op jit(solution)/shard_map/pallas_call | solution.py:405
  17.9 9.0 %shard_map.123 = (bf16[512,512]{1,0:T(8,128)(2,1)}, bf16[2048,512]{1,0:T(8,128)(2,1)}) custom-call(s32[16,128]{1,0:T(8,128)S(1)} %get-tuple-element.7.index_ref, f32[2048,512]{1,0:T(8,128)S(1)} %get-tuple-element.8.first_ref, f32[6656,128]{1,0:T(8,128)S(1)} %get-tuple-element.9.sent_ref, s32[16]{0:T(128)} %tile_hbm.3, bf16[2048,512]{1,0:T(8,128)(2,1)} %edge_hbm.3, ...), custom_call_target="tpu_custom_call" | custom-call | tf_op jit(solution)/shard_map/pallas_call | solution.py:589

commit v2 on v1

--- a/solution.py
+++ b/solution.py
@@ -16,11 +16,6 @@
 
 def dot(a, b):
     return jnp.dot(a, b, preferred_element_type=F32)
-
-
-def silu(value):
-    half = 0.5 * value
-    return half * (1.0 + jnp.tanh(half))
 
 
 def layer_norm(values, gain_vec):
@@ -96,20 +91,6 @@
     return jnp.where(sender < 0, 0, jnp.where(is_near, near_index, far_index))
 
 
-def border_hot(patch_rows, patch_cols, first_row, rows):
-    count = patch_rows * patch_cols
-    coarse_cols = patch_cols // 4
-    coarse = patch_rows // 4 * coarse_cols
-    pick = lax.broadcasted_iota(jnp.int32, (rows, count), 0) + first_row
-    node = lax.broadcasted_iota(jnp.int32, (rows, count), 1)
-    from_coarse = quotient(pick, coarse_cols) * (4 * patch_cols) + remainder(pick, coarse_cols) * 4
-    side = pick - coarse
-    from_side = jnp.where(
-        side < patch_rows, side * patch_cols, (side - patch_rows) * patch_cols + patch_cols - 1
-    )
-    return jnp.where(node == jnp.where(pick < coarse, from_coarse, from_side), 1.0, 0.0).astype(BF16)
-
-
 def gather_kernel(
     shape,
     patch_rows,
@@ -121,20 +102,32 @@
     recv_hbm,
     tile_hbm,
     w_hbm,
+    w_second_hbm,
+    edge_gain_hbm,
+    w_node_first_hbm,
+    w_node_second_hbm,
+    node_gain_hbm,
     first_ref,
     sent_ref,
     index_ref,
+    edge_ref,
+    recv_ref,
     own_ref,
-    edge_ref,
+    node_first_ref,
+    w_second_ref,
+    edge_gain_ref,
+    w_node_sum_ref,
+    w_node_second_ref,
+    node_gain_ref,
     send_ref,
-    recv_ref,
     tile_ref,
     w_ref,
+    w_node_own_ref,
+    flat_ref,
     side_ref,
     table_ref,
     received_ref,
     load_sem,
-    edge_sem,
     halo_send,
     halo_recv,
     line_send,
@@ -159,13 +152,24 @@
         return pltpu.make_async_copy(source, target, load_sem.at[i])
 
     loads = [
-        load(node_hbm, own_ref, 0),
-        load(w_hbm, w_ref, 1),
-        load(send_hbm, send_ref, 2),
-        load(recv_hbm, recv_ref, 3),
-        load(tile_hbm, tile_ref, 4),
+        load(source, target, i)
+        for i, (source, target) in enumerate(
+            (
+                (node_hbm, own_ref),
+                (w_hbm, w_ref),
+                (send_hbm, send_ref),
+                (recv_hbm, recv_ref),
+                (tile_hbm, tile_ref),
+                (edge_hbm, edge_ref),
+                (w_node_first_hbm.at[pl.ds(0, features), :], w_node_own_ref),
+                (w_node_first_hbm.at[pl.ds(features, features), :], w_node_sum_ref),
+                (w_second_hbm, w_second_ref),
+                (w_node_second_hbm, w_node_second_ref),
+                (edge_gain_hbm, edge_gain_ref),
+                (node_gain_hbm, node_gain_ref),
+            )
+        )
     ]
-    edge_load = pltpu.make_async_copy(edge_hbm, edge_ref, edge_sem)
     loads[0].start()
 
     def device(at_across, at_core, at_high, at_low):
@@ -210,10 +214,6 @@
         pl.semaphore_signal(
             barrier, inc=1, device_id=at, device_id_type=pl.DeviceIdType.MESH
         )
-    for each in loads[1:]:
-        each.start()
-    edge_load.start()
-
     def slots(at_high, at_core, at_across, at_low, count=1):
         block = ((at_high * cores + at_core) * wide + at_across) * low_count + at_low
         return pl.ds(pl.multiple_of(coarse_at + block * per, 8), count * per)
@@ -279,12 +279,30 @@
         origin = lat - halos[i][4]
         return (origin >= 0) & (origin < lat_count)
 
-    coarse_hot = border_hot(patch_rows, patch_cols, 0, per)
-    side_hot = border_hot(patch_rows, patch_cols, per, 2 * patch_rows)
+    def flatten(rows):
+        for t in range(tiles):
+            flat_ref[pl.ds(t * node_count + rows.start, rows.stop - rows.start), :] = own_ref[
+                rows, t * LANES : (t + 1) * LANES
+            ].astype(F32)
+
+    def picked(start, count, step):
+        parts = [
+            flat_ref[pl.ds(t * node_count + start, count, stride=step), :] for t in range(tiles)
+        ]
+        return jnp.concatenate(parts, axis=1).astype(BF16)
+
     loads[0].wait()
-    own = own_ref[...]
-    table_ref[slots(high, core, across, low), :] = dot(coarse_hot, own).astype(BF16)
-    side_ref[...] = dot(side_hot, own).astype(BF16)
+    coarse = []
+    for r in range(0, patch_rows, 4):
+        flatten(slice(r * patch_cols, (r + 1) * patch_cols))
+        coarse.append(picked(r * patch_cols, patch_cols // 4, 4))
+    table_ref[slots(high, core, across, low), :] = jnp.concatenate(coarse, axis=0)
+    for each in loads[1:]:
+        each.start()
+    for r in range(0, patch_rows, 4):
+        flatten(slice((r + 1) * patch_cols, (r + 4) * patch_cols))
+    side_ref[:patch_rows, :] = picked(0, patch_rows, patch_cols)
+    side_ref[patch_rows:, :] = picked(patch_cols - 1, patch_rows, patch_cols)
     for i, (_, _, size, target, _, _) in enumerate(halos):
 
         @pl.when(jnp.logical_not(receives(i)))
@@ -311,7 +329,7 @@
             pair(j, core).start()
 
     def project(rows, start):
-        result = dot(rows, w_ref[features : 2 * features, :])
+        result = 0.5 * dot(rows, w_ref[features : 2 * features, :])
         for t in range(tiles):
             sent_ref[pl.ds(start * tiles + t, rows.shape[0], stride=tiles), :] = result[
                 :, t * LANES : (t + 1) * LANES
@@ -337,20 +355,21 @@
                 for at in range(0, node_count, LANES)
             ]
             received.append(jnp.concatenate(parts, axis=1))
-        first_ref[rows, :] = dot(edge_ref[rows, :], w_ref[:features, :]) + dot(
+        result = dot(edge_ref[rows, :], w_ref[:features, :]) + dot(
             jnp.concatenate(received, axis=0), received_ref[...]
         )
+        first_ref[rows, :] = 0.5 * result
 
     loads[2].wait()
     index_ref[...] = tiles * sender_rows(
         send_ref[...], lat, lon, patch_rows, patch_cols, lon_count, shape
     )
     loads[1].wait()
-    received_ref[...] = dot(own, w_ref[2 * features :, :]).astype(BF16)
-    project(own, 0)
+    received_ref[...] = dot(own_ref[...], w_ref[2 * features :, :]).astype(BF16)
+    project(own_ref[...], 0)
     loads[3].wait()
     loads[4].wait()
-    edge_load.wait()
+    loads[5].wait()
 
     groups = 8 if blocks % 8 == 0 else 1
     size = blocks * block_len // groups
@@ -377,6 +396,10 @@
     do(len(work))
     project_coarse(high_count - 1)
 
+    loads[6].wait()
+    node_first_ref[...] = 0.5 * dot(own_ref[...], w_node_own_ref[...])
+    for each in loads[7:]:
+        each.wait()
     for k in range(1, high_count):
         line_out(k).wait_send()
     for j in range(high_count):
@@ -392,37 +415,45 @@
     return [pltpu.with_memory_space_constraint(each, pltpu.HBM) for each in arrays]
 
 
-def gather(shape, node, edges, senders, receivers, block_tile, w_first, patch_rows, patch_cols):
+def gather(shape, node, edges, senders, receivers, block_tile, weights, patch_rows, patch_cols):
     node_count, features = node.shape
     edge_count = edges.shape[0]
     blocks, block_len = receivers.shape
     tiles = features // LANES
-    near = shape["near"][-1] - node_count
     high = shape["high"]
     others = max(shape["wide"] * shape["low"] - 1, 1)
     dma = pltpu.SemaphoreType.DMA
     hbm, vmem = pl.BlockSpec(memory_space=pltpu.HBM), pl.BlockSpec(memory_space=pltpu.VMEM)
+    out_shape = [
+        pltpu.VMEM((edge_count, features), F32),
+        pltpu.VMEM((shape["length"] * tiles, LANES), F32),
+        pltpu.VMEM((blocks, block_len), jnp.int32),
+        pltpu.VMEM((edge_count, features), BF16),
+        pltpu.VMEM((blocks, block_len), jnp.int32),
+        pltpu.VMEM((node_count, features), BF16),
+        pltpu.VMEM((node_count, features), F32),
+        pltpu.VMEM((features, features), BF16),
+        pltpu.VMEM((1, features), F32),
+        pltpu.VMEM((features, features), BF16),
+        pltpu.VMEM((features, features), BF16),
+        pltpu.VMEM((1, features), F32),
+    ]
+    operands = (node, edges, senders, receivers, block_tile, *weights)
     return pl.pallas_call(
         functools.partial(gather_kernel, shape, patch_rows, patch_cols, 4 * patch_cols),
-        in_specs=[hbm] * 6,
-        out_specs=[vmem] * 3,
-        out_shape=[
-            pltpu.VMEM((edge_count, features), F32),
-            pltpu.VMEM((shape["length"] * tiles, LANES), F32),
-            pltpu.VMEM((blocks, block_len), jnp.int32),
-        ],
+        in_specs=[hbm] * len(operands),
+        out_specs=[vmem] * len(out_shape),
+        out_shape=out_shape,
         scratch_shapes=[
-            pltpu.VMEM((node_count, features), BF16),
-            pltpu.VMEM((edge_count, features), BF16),
-            pltpu.VMEM((blocks, block_len), jnp.int32),
             pltpu.VMEM((blocks, block_len), jnp.int32),
             pltpu.SMEM((blocks,), jnp.int32),
-            pltpu.VMEM(w_first.shape, BF16),
+            pltpu.VMEM(weights[0].shape, BF16),
+            pltpu.VMEM((features, features), BF16),
+            pltpu.VMEM((node_count * tiles, LANES), F32),
             pltpu.VMEM((2 * patch_rows, features), BF16),
             pltpu.VMEM((shape["length"] - node_count, features), BF16),
             pltpu.VMEM((node_count, features), BF16),
-            dma((5,)),
-            dma,
+            dma((12,)),
             dma((8,)),
             dma((8,)),
             dma((high,)),
@@ -433,40 +464,33 @@
             dma((high,)),
         ],
         compiler_params=pltpu.CompilerParams(
-            has_side_effects=True, collective_id=0, vmem_limit_bytes=20 * MIB
+            has_side_effects=True, collective_id=0, vmem_limit_bytes=16 * MIB
         ),
         cost_estimate=pl.CostEstimate(
             flops=8 * edge_count * features * features, bytes_accessed=8 * MIB, transcendentals=0
         ),
-    )(*in_hbm(node, edges, senders, receivers, block_tile, w_first))
+    )(*in_hbm(*operands))
 
 
 def update_kernel(
     group,
     tile_nodes,
+    tile_hbm,
     index_ref,
     first_ref,
     sent_ref,
-    tile_hbm,
-    edge_hbm,
-    recv_hbm,
-    node_hbm,
-    w_second_hbm,
-    edge_gain_hbm,
-    w_node_first_hbm,
-    w_node_second_hbm,
-    node_gain_hbm,
+    edge_ref,
+    recv_ref,
+    own_ref,
+    node_first_ref,
+    w_second_ref,
+    edge_gain_ref,
+    w_node_sum_ref,
+    w_node_second_ref,
+    node_gain_ref,
     node_out_hbm,
     edge_out_hbm,
     tile_ref,
-    edge_ref,
-    recv_ref,
-    own_ref,
-    w_second_ref,
-    edge_gain_ref,
-    w_node_first_ref,
-    w_node_second_ref,
-    node_gain_ref,
     picked_ref,
     hidden_ref,
     second_ref,
@@ -478,26 +502,12 @@
     out_sem,
 ):
     edge_count, features = edge_ref.shape
+    node_count = own_ref.shape[0]
     tiles = features // LANES
     block_len = recv_ref.shape[1]
     groups = edge_count // group
-    pairs = (
-        (w_second_hbm, w_second_ref),
-        (edge_gain_hbm, edge_gain_ref),
-        (edge_hbm, edge_ref),
-        (recv_hbm, recv_ref),
-        (tile_hbm, tile_ref),
-        (node_hbm, own_ref),
-        (w_node_first_hbm, w_node_first_ref),
-        (w_node_second_hbm, w_node_second_ref),
-        (node_gain_hbm, node_gain_ref),
-    )
-    loads = [
-        pltpu.make_async_copy(source, target, load_sem.at[i])
-        for i, (source, target) in enumerate(pairs)
-    ]
-    for each in loads:
-        each.start()
+    tile_load = pltpu.make_async_copy(tile_hbm, tile_ref, load_sem)
+    tile_load.start()
     total_ref[...] = jnp.zeros_like(total_ref)
 
     def pick(g):
@@ -513,11 +523,11 @@
             at = g * group + r
             parts = []
             for t in range(tiles):
-                first = (
+                half = (
                     first_ref[at : at + CHUNK, t * LANES : (t + 1) * LANES]
                     + picked_ref[slot, pl.ds(r * tiles + t, CHUNK, stride=tiles), :]
                 )
-                parts.append(silu(first).astype(BF16))
+                parts.append((half + half * jnp.tanh(half)).astype(BF16))
             hidden_ref[slot, r : r + CHUNK, :] = jnp.concatenate(parts, axis=1)
 
     def finish(g):
@@ -526,15 +536,15 @@
             block = g * (group // block_len) + i
             receiver = recv_ref[block : block + 1, :]
             spread = jnp.broadcast_to(receiver, (LANES, block_len)).T
+            live = jnp.where(spread >= 0, 1.0, 0.0).astype(BF16)
             for r in range(i * block_len, (i + 1) * block_len, CHUNK):
                 at = g * group + r
                 second = second_ref[slot, r : r + CHUNK, :]
                 message = layer_norm(second, edge_gain_ref[...]).astype(BF16)
                 message_ref[slot, r : r + CHUNK, :] = message
-                updated = edge_ref[at : at + CHUNK, :].astype(F32) + message.astype(F32)
-                live = spread[r % block_len : r % block_len + CHUNK, :]
-                live = jnp.concatenate([live] * tiles, axis=1)
-                edge_out_ref[at : at + CHUNK, :] = jnp.where(live >= 0, updated, 0.0).astype(BF16)
+                mask = live[r % block_len : r % block_len + CHUNK, :]
+                mask = jnp.concatenate([mask] * tiles, axis=1)
+                edge_out_ref[at : at + CHUNK, :] = (edge_ref[at : at + CHUNK, :] + message) * mask
             start = pl.multiple_of(tile_ref[block] * tile_nodes, tile_nodes)
             node = lax.broadcasted_iota(jnp.int32, (tile_nodes, block_len), 0)
             hot = jnp.where(node == receiver, 1.0, 0.0).astype(BF16)
@@ -551,25 +561,22 @@
     for g in range(groups):
         pick(g)
         hide(g)
-        if g == 0:
-            loads[0].wait()
         second_ref[g % 2] = dot(hidden_ref[g % 2], w_second_ref[...])
         if g == 0:
-            for each in loads[1:5]:
-                each.wait()
+            tile_load.wait()
         finish(g)
         store(g).start()
 
-    for each in loads[5:]:
-        each.wait()
-    own = own_ref[...]
-    node_first = dot(own, w_node_first_ref[:features, :]) + dot(
-        total_ref[...].astype(BF16), w_node_first_ref[features:, :]
-    )
-    node_second = dot(silu(node_first).astype(BF16), w_node_second_ref[...])
-    node_out_ref[...] = (
-        own.astype(F32) + layer_norm(node_second, node_gain_ref[...])
-    ).astype(BF16)
+    for at in range(0, node_count, tile_nodes):
+        rows = slice(at, at + tile_nodes)
+        half = node_first_ref[rows, :] + 0.5 * dot(
+            total_ref[rows, :].astype(BF16), w_node_sum_ref[...]
+        )
+        node_hidden = (half + half * jnp.tanh(half)).astype(BF16)
+        node_second = dot(node_hidden, w_node_second_ref[...])
+        node_out_ref[rows, :] = (
+            own_ref[rows, :].astype(F32) + layer_norm(node_second, node_gain_ref[...])
+        ).astype(BF16)
     node_store = pltpu.make_async_copy(node_out_ref, node_out_hbm, out_sem.at[groups])
     node_store.start()
     for g in range(groups):
@@ -577,26 +584,25 @@
     node_store.wait()
 
 
-def update(index, first, sent, block_tile, edges, receivers, node, weights, tile_nodes):
-    edge_count, features = edges.shape
-    node_count = node.shape[0]
-    blocks, block_len = receivers.shape
+def update(block_tile, gathered, tile_nodes):
+    edge_count, features = gathered[0].shape
+    node_count = gathered[5].shape[0]
+    blocks, block_len = gathered[4].shape
     tiles = features // LANES
     group = 4 * block_len if blocks % 4 == 0 else block_len
     groups = edge_count // group
     hbm, vmem = pl.BlockSpec(memory_space=pltpu.HBM), pl.BlockSpec(memory_space=pltpu.VMEM)
-    loaded = (edges, receivers, node, *weights)
+    first, sent, index, *rest = gathered
     return pl.pallas_call(
         functools.partial(update_kernel, group, tile_nodes),
-        in_specs=[pl.BlockSpec(memory_space=pltpu.SMEM), vmem, vmem] + [hbm] * 9,
+        in_specs=[hbm, pl.BlockSpec(memory_space=pltpu.SMEM)] + [vmem] * (2 + len(rest)),
         out_specs=[hbm, hbm],
         out_shape=[
             jax.ShapeDtypeStruct((node_count, features), BF16),
             jax.ShapeDtypeStruct((edge_count, features), BF16),
         ],
-        scratch_shapes=[pltpu.SMEM((blocks,), jnp.int32)]
-        + [pltpu.VMEM(each.shape, each.dtype) for each in loaded]
-        + [
+        scratch_shapes=[
+            pltpu.SMEM((blocks,), jnp.int32),
             pltpu.VMEM((2, group * tiles, LANES), F32),
             pltpu.VMEM((2, group, features), BF16),
             pltpu.VMEM((2, group, features), F32),
@@ -604,11 +610,11 @@
             pltpu.VMEM((edge_count, features), BF16),
             pltpu.VMEM((node_count, features), F32),
             pltpu.VMEM((node_count, features), BF16),
-            pltpu.SemaphoreType.DMA((9,)),
+            pltpu.SemaphoreType.DMA,
             pltpu.SemaphoreType.DMA((groups + 1,)),
         ],
-        compiler_params=pltpu.CompilerParams(vmem_limit_bytes=24 * MIB),
-    )(index, first, sent, *in_hbm(block_tile, *loaded))
+        compiler_params=pltpu.CompilerParams(vmem_limit_bytes=16 * MIB),
+    )(*in_hbm(block_tile), index, first, sent, *rest)
 
 
 def per_device(
@@ -628,28 +634,26 @@
     blocks = block_tile.shape[0]
     shape = plan(patch_rows, patch_cols, lax.axis_size("lat"), lax.axis_size("lon"))
     node = node_latent.reshape(patch_rows * patch_cols, features)
-    receivers = receiver.reshape(blocks, -1)
-    first, sent, index = gather(
-        shape,
-        node,
-        edge_latent,
-        sender.reshape(blocks, -1),
-        receivers,
-        block_tile,
+    weights = (
         w_first,
-        patch_rows,
-        patch_cols,
-    )
-    weights = (
         w_second,
         edge_gain.reshape(1, -1),
         w_node_first,
         w_node_second,
         node_gain.reshape(1, -1),
     )
-    node_out, edge_out = update(
-        index, first, sent, block_tile, edge_latent, receivers, node, weights, 4 * patch_cols
+    gathered = gather(
+        shape,
+        node,
+        edge_latent,
+        sender.reshape(blocks, -1),
+        receiver.reshape(blocks, -1),
+        block_tile,
+        weights,
+        patch_rows,
+        patch_cols,
     )
+    node_out, edge_out = update(block_tile, gathered, 4 * patch_cols)
     return node_out.reshape(patch_rows, patch_cols, features), edge_out
 
 

time: 27.1 us -> 26.6 us (0.982)
  Pallas kernels: 26.3 us -> 25.8 us
    pallas_call x1, Pallas kernels: 8.98 us -> 8.18 us  [update(): pl.pallas_call(functools.partial(update_kernel, group, tile_nodes), in_sp...]
    pallas_call x1, Pallas kernels: 17.3 us -> 17.6 us  [gather(): pl.pallas_call(functools.partial(gather_kernel, shape, patch_rows, patch_...]
where the time goes in v2:
time: 26.6 us; the launch traced here: 26.5 us
  Pallas kernels  25.8 us (97%)
  between operations  0.64 us (2%)
    pallas_call x1, Pallas kernels, gather(): pl.pallas_call(functools.partial(gather_kernel, shape, patch_rows, patch_...  17.6 us
    pallas_call x1, Pallas kernels, update(): pl.pallas_call(functools.partial(update_kernel, group, tile_nodes), in_sp...  8.18 us

profile of v2, /device:TPU:1, one launch (start us, length us, event | category | flops | bytes accessed | tf_op | source)
XLA Modules:
  0.0 26.5 jit_solution(15967254586341861997)
XLA Ops:
  0.6 17.6 %shard_map.122 = (f32[2048,512]{1,0:T(8,128)S(1)}, f32[6656,128]{1,0:T(8,128)S(1)}, s32[16,128]{1,0:T(8,128)S(1)}, bf16[2048,512]{1,0:T(8,128)(2,1)S(1)}, s32[16...) custom-call(bf16[512,512]{1,0:T(8,128)(2,1)} %bitcast.6, ...), custom_call_target="tpu_custom_call" | custom-call | flops 4294967296 | bytes 8388608 | tf_op jit(solution)/shard_map/pallas_call | solution.py:442
  18.3 8.2 %shard_map.123 = (bf16[512,512]{1,0:T(8,128)(2,1)}, bf16[2048,512]{1,0:T(8,128)(2,1)}) custom-call(s32[16]{0:T(128)} %tile_hbm.3, s32[16,128]{1,0:T(8,128)S(1)} %get-tuple-element.16.index_ref, f32[2048,512]{1,0:T(8,128)S(1)} %get-tuple-element.17.first_ref, f32[6656,128]{1,0:T(8,128)S(1)} %get-tuple-element.18.sent_ref, ...), custom_call_target="tpu_custom_call" | custom-call | tf_op jit(solution)/shard_map/pallas_call | solution.py:596

commit v3 on v2

--- a/solution.py
+++ b/solution.py
@@ -110,6 +110,7 @@
     first_ref,
     sent_ref,
     index_ref,
+    tile_ref,
     edge_ref,
     recv_ref,
     own_ref,
@@ -120,13 +121,14 @@
     w_node_second_ref,
     node_gain_ref,
     send_ref,
-    tile_ref,
+    rows_ref,
     w_ref,
     w_node_own_ref,
     flat_ref,
     side_ref,
     table_ref,
     received_ref,
+    index_sem,
     load_sem,
     halo_send,
     halo_recv,
@@ -170,7 +172,8 @@
             )
         )
     ]
-    loads[0].start()
+    for each in loads[:2]:
+        each.start()
 
     def device(at_across, at_core, at_high, at_low):
         return at_across * cores + at_core, at_high * low_count + at_low
@@ -297,7 +300,7 @@
         flatten(slice(r * patch_cols, (r + 1) * patch_cols))
         coarse.append(picked(r * patch_cols, patch_cols // 4, 4))
     table_ref[slots(high, core, across, low), :] = jnp.concatenate(coarse, axis=0)
-    for each in loads[1:]:
+    for each in loads[2:]:
         each.start()
     for r in range(0, patch_rows, 4):
         flatten(slice((r + 1) * patch_cols, (r + 4) * patch_cols))
@@ -310,16 +313,22 @@
             table_ref[target : target + size, :] = jnp.zeros((size, features), BF16)
 
     pl.semaphore_wait(barrier, len(greeted))
-    for k in range(1, high_count):
-        line_out(k).start()
-    for i in range(len(offsets)):
+    for h in range(high_count):
+
+        @pl.when(high == h)
+        def _():
+            for at in sorted(range(high_count), key=lambda at: -abs(at - h)):
+                if at != h:
+                    line_out((at - h) % high_count).start()
+
+    for i in reversed(range(len(offsets))):
         plane_out(0, i).start()
     for i in range(len(halos)):
         pl.when(sends(i))(lambda i=i: halo(i).start())
 
     def relay_line(k):
         line_in(k).wait_recv()
-        for i in range(len(offsets)):
+        for i in reversed(range(len(offsets))):
             plane_out(k, i).start()
 
     def relay_plane(j):
@@ -361,7 +370,7 @@
         first_ref[rows, :] = 0.5 * result
 
     loads[2].wait()
-    index_ref[...] = tiles * sender_rows(
+    rows_ref[...] = tiles * sender_rows(
         send_ref[...], lat, lon, patch_rows, patch_cols, lon_count, shape
     )
     loads[1].wait()
@@ -379,27 +388,26 @@
         for _ in range(min(count, len(work))):
             work.pop(0)()
 
+    do(2)
     for k in range(1, high_count):
         relay_line(k)
         do(1)
     relay_plane(0)
-    do(2)
+    index_copy = pltpu.make_async_copy(rows_ref, index_ref, index_sem)
+    index_copy.start()
+    do(len(work))
+    loads[6].wait()
+    node_first_ref[...] = 0.5 * dot(own_ref[...], w_node_own_ref[...])
+    for i in range(len(halos)):
+        pl.when(receives(i))(lambda i=i: halo(i).wait_recv())
+    project(table_ref[:coarse_at, :], node_count)
     for j in range(1, high_count):
         relay_plane(j)
-        do(1)
-        if j == 1:
-            do(len(work))
-            for i in range(len(halos)):
-                pl.when(receives(i))(lambda i=i: halo(i).wait_recv())
-            project(table_ref[:coarse_at, :], node_count)
         project_coarse(j - 1)
-    do(len(work))
     project_coarse(high_count - 1)
-
-    loads[6].wait()
-    node_first_ref[...] = 0.5 * dot(own_ref[...], w_node_own_ref[...])
     for each in loads[7:]:
         each.wait()
+    index_copy.wait()
     for k in range(1, high_count):
         line_out(k).wait_send()
     for j in range(high_count):
@@ -424,10 +432,12 @@
     others = max(shape["wide"] * shape["low"] - 1, 1)
     dma = pltpu.SemaphoreType.DMA
     hbm, vmem = pl.BlockSpec(memory_space=pltpu.HBM), pl.BlockSpec(memory_space=pltpu.VMEM)
+    smem = pl.BlockSpec(memory_space=pltpu.SMEM)
     out_shape = [
         pltpu.VMEM((edge_count, features), F32),
         pltpu.VMEM((shape["length"] * tiles, LANES), F32),
-        pltpu.VMEM((blocks, block_len), jnp.int32),
+        pltpu.SMEM((blocks, block_len), jnp.int32),
+        pltpu.SMEM((blocks,), jnp.int32),
         pltpu.VMEM((edge_count, features), BF16),
         pltpu.VMEM((blocks, block_len), jnp.int32),
         pltpu.VMEM((node_count, features), BF16),
@@ -442,17 +452,18 @@
     return pl.pallas_call(
         functools.partial(gather_kernel, shape, patch_rows, patch_cols, 4 * patch_cols),
         in_specs=[hbm] * len(operands),
-        out_specs=[vmem] * len(out_shape),
+        out_specs=[vmem] * 2 + [smem] * 2 + [vmem] * 9,
         out_shape=out_shape,
         scratch_shapes=[
             pltpu.VMEM((blocks, block_len), jnp.int32),
-            pltpu.SMEM((blocks,), jnp.int32),
+            pltpu.VMEM((blocks, block_len), jnp.int32),
             pltpu.VMEM(weights[0].shape, BF16),
             pltpu.VMEM((features, features), BF16),
             pltpu.VMEM((node_count * tiles, LANES), F32),
             pltpu.VMEM((2 * patch_rows, features), BF16),
             pltpu.VMEM((shape["length"] - node_count, features), BF16),
             pltpu.VMEM((node_count, features), BF16),
+            dma,
             dma((12,)),
             dma((8,)),
             dma((8,)),
@@ -475,10 +486,10 @@
 def update_kernel(
     group,
     tile_nodes,
-    tile_hbm,
-    index_ref,
     first_ref,
     sent_ref,
+    index_ref,
+    tile_ref,
     edge_ref,
     recv_ref,
     own_ref,
@@ -490,7 +501,6 @@
     node_gain_ref,
     node_out_hbm,
     edge_out_hbm,
-    tile_ref,
     picked_ref,
     hidden_ref,
     second_ref,
@@ -498,7 +508,6 @@
     edge_out_ref,
     total_ref,
     node_out_ref,
-    load_sem,
     out_sem,
 ):
     edge_count, features = edge_ref.shape
@@ -506,8 +515,6 @@
     tiles = features // LANES
     block_len = recv_ref.shape[1]
     groups = edge_count // group
-    tile_load = pltpu.make_async_copy(tile_hbm, tile_ref, load_sem)
-    tile_load.start()
     total_ref[...] = jnp.zeros_like(total_ref)
 
     def pick(g):
@@ -558,12 +565,18 @@
             edge_out_ref.at[rows, :], edge_out_hbm.at[rows, :], out_sem.at[g]
         )
 
+    def node_store(at):
+        rows = pl.ds(at, tile_nodes)
+        return pltpu.make_async_copy(
+            node_out_ref.at[rows, :],
+            node_out_hbm.at[rows, :],
+            out_sem.at[groups + at // tile_nodes],
+        )
+
     for g in range(groups):
         pick(g)
         hide(g)
         second_ref[g % 2] = dot(hidden_ref[g % 2], w_second_ref[...])
-        if g == 0:
-            tile_load.wait()
         finish(g)
         store(g).start()
 
@@ -577,32 +590,31 @@
         node_out_ref[rows, :] = (
             own_ref[rows, :].astype(F32) + layer_norm(node_second, node_gain_ref[...])
         ).astype(BF16)
-    node_store = pltpu.make_async_copy(node_out_ref, node_out_hbm, out_sem.at[groups])
-    node_store.start()
+        node_store(at).start()
     for g in range(groups):
         store(g).wait()
-    node_store.wait()
-
-
-def update(block_tile, gathered, tile_nodes):
+    for at in range(0, node_count, tile_nodes):
+        node_store(at).wait()
+
+
+def update(gathered, tile_nodes):
     edge_count, features = gathered[0].shape
-    node_count = gathered[5].shape[0]
-    blocks, block_len = gathered[4].shape
+    blocks, block_len = gathered[2].shape
+    node_count = gathered[6].shape[0]
     tiles = features // LANES
     group = 4 * block_len if blocks % 4 == 0 else block_len
     groups = edge_count // group
     hbm, vmem = pl.BlockSpec(memory_space=pltpu.HBM), pl.BlockSpec(memory_space=pltpu.VMEM)
-    first, sent, index, *rest = gathered
+    smem = pl.BlockSpec(memory_space=pltpu.SMEM)
     return pl.pallas_call(
         functools.partial(update_kernel, group, tile_nodes),
-        in_specs=[hbm, pl.BlockSpec(memory_space=pltpu.SMEM)] + [vmem] * (2 + len(rest)),
+        in_specs=[vmem] * 2 + [smem] * 2 + [vmem] * (len(gathered) - 4),
         out_specs=[hbm, hbm],
         out_shape=[
             jax.ShapeDtypeStruct((node_count, features), BF16),
             jax.ShapeDtypeStruct((edge_count, features), BF16),
         ],
         scratch_shapes=[
-            pltpu.SMEM((blocks,), jnp.int32),
             pltpu.VMEM((2, group * tiles, LANES), F32),
             pltpu.VMEM((2, group, features), BF16),
             pltpu.VMEM((2, group, features), F32),
@@ -610,11 +622,10 @@
             pltpu.VMEM((edge_count, features), BF16),
             pltpu.VMEM((node_count, features), F32),
             pltpu.VMEM((node_count, features), BF16),
-            pltpu.SemaphoreType.DMA,
-            pltpu.SemaphoreType.DMA((groups + 1,)),
+            pltpu.SemaphoreType.DMA((groups + node_count // tile_nodes,)),
         ],
         compiler_params=pltpu.CompilerParams(vmem_limit_bytes=16 * MIB),
-    )(*in_hbm(block_tile), index, first, sent, *rest)
+    )(*gathered)
 
 
 def per_device(
@@ -653,7 +664,7 @@
         patch_rows,
         patch_cols,
     )
-    node_out, edge_out = update(block_tile, gathered, 4 * patch_cols)
+    node_out, edge_out = update(gathered, 4 * patch_cols)
     return node_out.reshape(patch_rows, patch_cols, features), edge_out
 
 

time: 26.6 us -> 25.2 us (0.947)
  the two profiles are of different devices: /device:TPU:1 before, /device:TPU:11 now
where the time goes in v3:
time: 25.2 us; the launch traced here: 25 us
  Pallas kernels  24.4 us (97%)
  between operations  0.64 us (3%)
    pallas_call x1, Pallas kernels, gather(): pl.pallas_call(functools.partial(gather_kernel, shape, patch_rows, patch_...  17.4 us
    pallas_call x1, Pallas kernels, update(): pl.pallas_call(functools.partial(update_kernel, group, tile_nodes), in_sp...  7.03 us

profile of v3, /device:TPU:11, one launch (start us, length us, event | category | flops | bytes accessed | tf_op | source)
XLA Modules:
  0.0 25.0 jit_solution(309227361244151247)
XLA Ops:
  0.6 17.4 %shard_map.122 = (f32[2048,512]{1,0:T(8,128)S(1)}, f32[6656,128]{1,0:T(8,128)S(1)}, s32[16,128]{1,0:T(8,128)S(4)}, s32[16]{0:T(128)S(4)}, bf16[2048,512]{1,0:T(8...) custom-call(bf16[512,512]{1,0:T(8,128)(2,1)} %bitcast.6, ...), custom_call_target="tpu_custom_call" | custom-call | flops 4294967296 | bytes 8388608 | tf_op jit(solution)/shard_map/pallas_call | solution.py:452
  18.0 7.0 %shard_map.123 = (bf16[512,512]{1,0:T(8,128)(2,1)}, bf16[2048,512]{1,0:T(8,128)(2,1)}) custom-call(f32[2048,512]{1,0:T(8,128)S(1)} %get-tuple-element.17.first_ref, f32[6656,128]{1,0:T(8,128)S(1)} %get-tuple-element.18.sent_ref, s32[16,128]{1,0:T(8,128)S(4)} %get-tuple-element.19.index_ref, s32[16]{0:T(128)S(4)} %get-tuple-element.20.tile_ref, ...), custom_call_target="tpu_custom_call" | custom-call | tf_op jit(solution)/shard_map/pallas_call | solution.py:609

commit v4 on v3

--- a/solution.py
+++ b/solution.py
@@ -602,7 +602,7 @@
     blocks, block_len = gathered[2].shape
     node_count = gathered[6].shape[0]
     tiles = features // LANES
-    group = 4 * block_len if blocks % 4 == 0 else block_len
+    group = 8 * block_len if blocks % 8 == 0 else block_len
     groups = edge_count // group
     hbm, vmem = pl.BlockSpec(memory_space=pltpu.HBM), pl.BlockSpec(memory_space=pltpu.VMEM)
     smem = pl.BlockSpec(memory_space=pltpu.SMEM)
@@ -624,7 +624,7 @@
             pltpu.VMEM((node_count, features), BF16),
             pltpu.SemaphoreType.DMA((groups + node_count // tile_nodes,)),
         ],
-        compiler_params=pltpu.CompilerParams(vmem_limit_bytes=16 * MIB),
+        compiler_params=pltpu.CompilerParams(vmem_limit_bytes=28 * MIB),
     )(*gathered)
 
 

time: 25.2 us -> 24.8 us (0.984)
  Pallas kernels: 24.4 us -> 24 us
    pallas_call x1, Pallas kernels: 7.03 us -> 6.68 us  [update(): pl.pallas_call(functools.partial(update_kernel, group, tile_nodes), in_sp...]
where the time goes in v4:
time: 24.8 us; the launch traced here: 24.7 us
  Pallas kernels  24 us (97%)
  between operations  0.64 us (3%)
    pallas_call x1, Pallas kernels, gather(): pl.pallas_call(functools.partial(gather_kernel, shape, patch_rows, patch_...  17.4 us
    pallas_call x1, Pallas kernels, update(): pl.pallas_call(functools.partial(update_kernel, group, tile_nodes), in_sp...  6.68 us

profile of v4, /device:TPU:11, one launch (start us, length us, event | category | flops | bytes accessed | tf_op | source)
XLA Modules:
  0.0 24.7 jit_solution(10147553015612276932)
XLA Ops:
  0.6 17.4 %shard_map.122 = (f32[2048,512]{1,0:T(8,128)S(1)}, f32[6656,128]{1,0:T(8,128)S(1)}, s32[16,128]{1,0:T(8,128)S(4)}, s32[16]{0:T(128)S(4)}, bf16[2048,512]{1,0:T(8...) custom-call(bf16[512,512]{1,0:T(8,128)(2,1)} %bitcast.6, ...), custom_call_target="tpu_custom_call" | custom-call | flops 4294967296 | bytes 8388608 | tf_op jit(solution)/shard_map/pallas_call | solution.py:452
  18.0 6.7 %shard_map.123 = (bf16[512,512]{1,0:T(8,128)(2,1)}, bf16[2048,512]{1,0:T(8,128)(2,1)}) custom-call(f32[2048,512]{1,0:T(8,128)S(1)} %get-tuple-element.17.first_ref, f32[6656,128]{1,0:T(8,128)S(1)} %get-tuple-element.18.sent_ref, s32[16,128]{1,0:T(8,128)S(4)} %get-tuple-element.19.index_ref, s32[16]{0:T(128)S(4)} %get-tuple-element.20.tile_ref, ...), custom_call_target="tpu_custom_call" | custom-call | tf_op jit(solution)/shard_map/pallas_call | solution.py:609
